TPU v7x, 32 devices: a whole 2x2x4 slice. The times are simulated.
32 devices in a mesh: light: 4 (over y, x), screen: 8 (over z, core).
Axes of the slice: x: 2, y: 2, z: 4, core: 2. Of those that a mesh axis runs over, the one named last changes fastest.
Arguments:
- density: float32 [128, 256, 512], P('screen', None, 'light'), may hold values from 0 to 1.09375, as said below
- albedo: float32 [128, 256, 512], P('screen', None, 'light'), may hold values from 0.2 to 1
- light_in: float32 [128, 256], replicated, may hold values from 0.5 to 1.5
- occupancy: int32 [8, 16, 32], P('screen', None, 'light'), may hold values 0 or 1
- phase: int32 [256, 512], replicated, may hold values from 0 to 15
- fractions: float32 [3, 16], replicated, may hold values from 0 to 1
Outputs:
- image: float32 [256, 512], P('screen', 'light')
- transmittance: float32 [256, 512], P('screen', 'light')
- lit_bricks: float32 [128, 256, 512], P('light', 'screen')
Inputs may be any that keep to these rules, and one draw needn't show every extreme that they name: `density`: nonnegative extinction of each cell. `occupancy`: 1 where the brick of 16 cells on a side is occupied.
All inputs are finite; a program needn't handle non-finite values. No bound on the sum of `occupancy` on one device may be relied on, other than what follows from the above.
Results may differ from a plain program's by a relative error of at most 0.0003.
Values sent between devices are 32-bit elements; how exact they have to be, the bound alone decides.
No kernel may reach another device: no remote copies, remote signals or barrier semaphores. Data moves between devices by JAX's collectives and lax.ppermute only.
A program may use at most 192 MiB of HBM per device.

v0:
```python
import jax
import jax.numpy as jnp
from jax import lax
from jax.sharding import PartitionSpec as P

BRICK = 16


def passed_along(value, axis, by):
    peers = lax.axis_size(axis)
    pairs = [(i, i + by) for i in range(peers) if 0 <= i + by < peers]
    return lax.ppermute(value, axis, pairs)


def carried_in(part, axis, combine, identity):
    place = lax.axis_index(axis)
    gathered = lax.all_gather(part, axis)
    state = jnp.zeros_like(part) + jnp.asarray(identity, part.dtype)

    def one(step, state):
        return combine(state, lax.dynamic_index_in_dim(gathered, step, 0, False))

    return lax.fori_loop(0, place, one, state)


def prefix_last(values):
    length = values.shape[-1]
    block = 128
    count = length // block
    shaped = values.reshape(values.shape[:-1] + (count, block))
    rowsidx = lax.broadcasted_iota(jnp.int32, (block, block), 0)
    colsidx = lax.broadcasted_iota(jnp.int32, (block, block), 1)
    upper = (rowsidx < colsidx).astype(jnp.float32)
    within = jnp.matmul(shaped, upper, precision=lax.Precision.HIGHEST)
    totals = jnp.sum(shaped, axis=-1)
    carried = jnp.cumsum(totals, axis=-1) - totals
    return (within + carried[..., None]).reshape(values.shape)


def prefix_first(values):
    length = values.shape[0]
    count = length // length
    shaped = values.reshape(count, length, -1)
    rowsidx = lax.broadcasted_iota(jnp.int32, (length, length), 0)
    colsidx = lax.broadcasted_iota(jnp.int32, (length, length), 1)
    lower = (colsidx < rowsidx).astype(jnp.float32)
    within = jnp.einsum("ij,bjr->bir", lower, shaped, precision=lax.Precision.HIGHEST)
    totals = jnp.sum(shaped, axis=1)
    carried = jnp.cumsum(totals, axis=0) - totals
    return (within + carried[:, None]).reshape(values.shape)


def corner_fractions(rays, fractions):
    levels = lax.broadcasted_iota(jnp.int32, (fractions.shape[1], 1, 1), 0)
    onehot = (rays[None] == levels).astype(jnp.float32)
    return jnp.einsum("kp,prc->krc", fractions, onehot, precision=lax.Precision.HIGHEST)


def resample(field, tail, weights, deep, cols):
    first = field[:, 0:cols]
    second = field[:, 1 : cols + 1]
    edge_first = tail[:, 0:cols]
    edge_second = tail[:, 1 : cols + 1]
    first_next = jnp.concatenate([first[:, :, 1:], edge_first], axis=2)
    second_next = jnp.concatenate([second[:, :, 1:], edge_second], axis=2)
    depth_w = weights[0]
    column_w = weights[1]
    light_w = weights[2]
    near = first + column_w * (second - first)
    further = first_next + column_w * (second_next - first_next)
    mixed = near + light_w * (further - near)
    lower = mixed[0:deep]
    higher = mixed[1 : deep + 1]
    return lower + depth_w * (higher - lower)


def composite(extinct, shaded):
    screened = prefix_first(extinct)
    part = jnp.sum(jnp.exp(-screened) * (1.0 - jnp.exp(-extinct)) * shaded, axis=0)
    return (part, jnp.sum(extinct, axis=0))


def finish(parts, totals):
    before = jnp.cumsum(totals, axis=0) - totals
    picture = jnp.sum(jnp.exp(-before) * parts, axis=0)
    return (picture, jnp.exp(-jnp.sum(totals, axis=0)))


def march_slabs(masked, lit, phase, fractions):
    slab_b, width_a, slab_l = masked.shape
    light_idx = lax.axis_index("light")
    rims = passed_along((masked[:2], lit[:2]), "screen", -1)
    dens_ext = jnp.pad(jnp.concatenate([masked, rims[0]], axis=0), ((0, 0), (0, 2), (0, 0)))
    lit_ext = jnp.pad(jnp.concatenate([lit, rims[1]], axis=0), ((0, 0), (0, 2), (0, 0)))
    tails = passed_along((dens_ext[:, :, :1], lit_ext[:, :, :1]), "light", -1)
    rays = lax.dynamic_slice_in_dim(phase, light_idx * slab_l, slab_l, 1)
    weights = corner_fractions(rays, fractions)
    extinct = resample(dens_ext, tails[0], weights, slab_b, width_a)
    shaded = resample(lit_ext, tails[1], weights, slab_b, width_a)
    part, total = composite(extinct, shaded)
    parts, totals = (
        lax.all_to_all(part[None], "screen", split_axis=1, concat_axis=0, tiled=True),
        lax.all_to_all(total[None], "screen", split_axis=1, concat_axis=0, tiled=True),
    )
    return finish(parts, totals)


def local(density, albedo, light_in, occupancy, phase, fractions):
    slab_b, width_a, slab_l = density.shape
    bricks_b, bricks_a, bricks_l = occupancy.shape
    masked = (
        density.reshape(bricks_b, BRICK, bricks_a, BRICK, bricks_l, BRICK)
        * occupancy.astype(jnp.float32)[:, None, :, None, :, None]
    ).reshape(density.shape)
    screen_idx = lax.axis_index("screen")
    local_depth = prefix_last(masked)
    totals = jnp.sum(masked, axis=2)
    before = carried_in(totals, "light", jnp.add, jnp.zeros_like(totals))
    incoming = lax.dynamic_slice_in_dim(light_in, screen_idx * slab_b, slab_b, 0)
    lit = albedo * incoming[:, :, None] * jnp.exp(-(local_depth + before[:, :, None]))
    lit_cam = lax.all_to_all(lit, "screen", split_axis=1, concat_axis=0, tiled=True)
    lit_cam = lax.all_to_all(lit_cam, "light", split_axis=0, concat_axis=2, tiled=True)
    picture, passing = march_slabs(masked, lit, phase, fractions)
    return (picture, passing, lit_cam)


def solution(mesh):
    return jax.shard_map(
        local,
        mesh=mesh,
        in_specs=(
            P("screen", None, "light"),
            P("screen", None, "light"),
            P(),
            P("screen", None, "light"),
            P(),
            P(),
        ),
        out_specs=(P("screen", "light"), P("screen", "light"), P("light", "screen", None)),
        check_vma=False,
    )
```

profile of v0, /device:TPU:0, one launch (start us, length us, event | category | flops | bytes accessed | tf_op | source)
XLA Modules:
  0.0 195.5 jit_solution(17380704200879934052)
XLA Ops:
  0.7 0.7 convert_bitcast_fusion
  1.9 2.2 %fusion.35 = (f32[16,256]{1,0:T(8,128)S(1)}, f32[16,256,128]{2,1,0:T(8,128)S(1)}) fusion(f32[16,256,128]{2,1,0:T(8,128)} %param.8, f32[256,128]{1,0:T(8,128)S(1)} %mul.121), kind=kLoop, calls=%fused_computation.62 | loop fusion | flops 1044480 | bytes 4341760 | tf_op jit(solution)/shard_map/reduce_sum | solution.py:35
  4.2 9.7 %all-gather = f32[64,256]{1,0:T(8,128)S(1)} all-gather(f32[16,256]{1,0:T(8,128)S(1)} %get-tuple-element.35), channel_id=2, replica_groups=mesh['light'=4,'screen'=8] {'light'}, dimensions={0}, use_global_device_ids=true | all-gather | bytes 81920 | tf_op jit(solution)/shard_map/all_gather | solution.py:17
  13.9 0.7 constant_dynamic-slice_fusion
  14.6 3.8 %exponential_multiply_fusion = f32[16,256,128]{2,1,0:T(8,128)S(1)} fusion(f32[16,256,128]{2,1,0:T(8,128)} %param.9, f32[16,256,128]{2,1,0:T(8,128)S(1)} %get-tuple-element.36, f32[16,256]{1,0:T(8,128)S(1)} %get-tuple-element.26, f32[16,256]{1,0:T(8,128)S(1)} %sub.66, f32[16,256]{1,0:T(8,128)S(1)} %constant_dynamic-slice_fusion), kind=kOutput, calls=%fused_computation.42 | convolution fusion | flops 807944192 | bytes 6340608 | tf_op jit(solution)/shard_map/dot_general | solution.py:34
  18.5 1.3 copy-done.3
  19.8 1.3 collective-permute-start.2
  21.1 10.6 %reshape.82 = f32[1,16,16,16,8,16]{5,4,3,2,1,0:T(8,128)} reshape(f32[16,256,128]{2,1,0:T(8,128)} %param.8) | data formatting | bytes 4194304 | tf_op jit(solution)/shard_map/reshape | solution.py:112
  31.7 1.9 slice_multiply_fusion
  33.6 1.3 slice.74
  34.8 1.3 collective-permute-start
  36.2 0.7 fusion.27
  36.9 1.0 fusion.38
  37.9 1.7 pad_maximum_fusion.1
  39.6 2.1 %pad_slice_fusion.2 = f32[18,256,127]{2,1,0:T(8,128)} fusion(f32[18,256,128]{2,1,0:T(8,128)S(1)} %pad_maximum_fusion.1), kind=kLoop, calls=%fused_computation.25 | loop fusion | bytes 4700160 | tf_op jit(solution)/shard_map/slice | solution.py:65
  41.7 1.6 pad_slice_fusion.3
  43.4 0.9 copy-done.6
  44.4 2.2 %pad_slice_fusion.4 = f32[18,256,127]{2,1,0:T(8,128)} fusion(f32[18,256,128]{2,1,0:T(8,128)S(1)} %pad_maximum_fusion), kind=kLoop, calls=%fused_computation.27 | loop fusion | bytes 4700160 | tf_op jit(solution)/shard_map/slice | solution.py:65
  46.6 1.6 pad_slice_fusion.5
  48.2 2.7 %copy.33 = f32[18,258,1]{1,2,0:T(1,128)S(1)} copy(f32[18,258,1]{2,1,0:T(8,128)} %pad_slice_fusion.3) | data formatting | bytes 37152 | tf_op jit(solution)/shard_map/slice | solution.py:95
  50.9 1.3 collective-permute-start.3
  52.2 2.7 %copy.30 = f32[18,258,1]{1,2,0:T(1,128)S(1)} copy(f32[18,258,1]{2,1,0:T(8,128)} %pad_slice_fusion.5) | data formatting | bytes 37152 | tf_op jit(solution)/shard_map/slice | solution.py:95
  54.9 1.6 collective-permute-start.1
  56.5 3.7 %fusion.3 = f32[18,256,127]{2,1,0:T(8,128)} fusion(f32[2,256,128]{2,1,0:T(8,128)S(1)} %collective-permute-done.2, f32[16,256,128]{2,1,0:T(8,128)} %copy-done.3), kind=kLoop, calls=%fused_computation.9 | loop fusion | flops 585216 | bytes 4700160 | tf_op jit(solution)/shard_map/concatenate | solution.py:94
  60.2 2.1 %fusion.4 = f32[18,256,127]{2,1,0:T(8,128)} fusion(f32[2,256,128]{2,1,0:T(8,128)S(1)} %collective-permute-done, f32[16,256,128]{2,1,0:T(8,128)S(1)} %copy-done.7), kind=kLoop, calls=%fused_computation.10 | loop fusion | flops 585216 | bytes 4700160 | tf_op jit(solution)/shard_map/concatenate | solution.py:93
  62.4 2.1 %copy.35 = f32[18,256,1]{2,1,0:T(8,128)} copy(f32[18,256,1]{1,2,0:T(1,128)S(1)} %get-tuple-element.44) | data formatting | bytes 36864 | tf_op jit(solution)/shard_map/slice | solution.py:63
  64.6 2.2 %copy.34 = f32[18,256,1]{2,1,0:T(8,128)} copy(f32[18,256,1]{1,2,0:T(1,128)S(1)} %get-tuple-element.45) | data formatting | bytes 36864 | tf_op jit(solution)/shard_map/slice | solution.py:62
  66.8 2.1 %copy.32 = f32[18,256,1]{2,1,0:T(8,128)} copy(f32[18,256,1]{1,2,0:T(1,128)S(1)} %get-tuple-element.46) | data formatting | bytes 36864 | tf_op jit(solution)/shard_map/slice | solution.py:63
  69.0 2.1 %copy.31 = f32[18,256,1]{2,1,0:T(8,128)} copy(f32[18,256,1]{1,2,0:T(1,128)S(1)} %get-tuple-element.47) | data formatting | bytes 36864 | tf_op jit(solution)/shard_map/slice | solution.py:62
  71.1 12.0 %fusion.14 = (f32[18,256,128]{2,1,0:T(8,128)}, f32[18,256,128]{2,1,0:T(8,128)S(1)}) fusion(f32[18,256,1]{2,1,0:T(8,128)} %copy.34, f32[18,256,127]{2,1,0:T(8,128)} %fusion.3, f32[18,256,1]{2,1,0:T(8,128)} %copy.35, f32[18,256,127]{2,1,0:T(8,128)} %pad_slice_fusion.2, f32[18,256,128]{2,1,0:T(8,128)S(1)} %pad_maximum_fusion.1, f32[256,128]{1,0:T(8,128)S(1)} %bitcast.74, ...), kind=kLoop, calls=%fused_computation.24 | loop fusion | flops 12976128 | bytes 19136512 | tf_op jit(solution)/shard_map/add | solution.py:71
  83.2 2.3 %fusion.36 = (f32[256,128]{1,0:T(8,128)}, f32[16,256,128]{2,1,0:T(8,128)}) fusion(f32[18,256,128]{2,1,0:T(8,128)S(1)} %get-tuple-element.43, f32[256,128]{1,0:T(8,128)S(1)} %bitcast.72), kind=kLoop, calls=%fused_computation.63 | loop fusion | flops 2064384 | bytes 6553600 | tf_op jit(solution)/shard_map/reduce_sum | solution.py:80
  85.5 6.7 %all-to-all-start = ((f32[1,256,128]{2,0,1:T(1,128)}), f32[1,256,128]{2,0,1:T(1,128)S(1)}, u32[]{:S(2)}, u32[]{:S(2)}) async-start(f32[1,256,128]{2,0,1:T(1,128)} %bitcast.7), calls=%async_computation | async-start | bytes 262144 | tf_op jit(solution)/shard_map/all_to_all | solution.py:103
  92.2 2.5 %copy.36 = f32[16,256,128]{2,0,1:T(8,128)} copy(f32[16,256,128]{2,1,0:T(8,128)S(1)} %copy-done.4) | data formatting | bytes 4194304 | tf_op jit(solution)/shard_map/mul | solution.py:120
  94.7 4.2 %all-to-all-done = f32[1,256,128]{2,0,1:T(1,128)S(1)} async-done(((f32[1,256,128]{2,0,1:T(1,128)}), f32[1,256,128]{2,0,1:T(1,128)S(1)}, u32[]{:S(2)}, u32[]{:S(2)}) %all-to-all-start) | async-done | bytes 131104 | tf_op jit(solution)/shard_map/all_to_all | solution.py:103
  98.9 4.4 %all-to-all-start.2 = ((f32[16,256,128]{2,0,1:T(8,128)}), f32[16,256,128]{2,0,1:T(8,128)}, u32[]{:S(2)}, u32[]{:S(2)}) async-start(f32[16,256,128]{2,0,1:T(8,128)} %copy.36), calls=%async_computation.2 | async-start | bytes 4194304 | tf_op jit(solution)/shard_map/all_to_all | solution.py:121
  103.3 0.9 subtract_bitcast_fusion
  104.2 2.5 %fusion.24 = f32[2,8,256,128]{3,1,2,0:T(8,128)S(1)} fusion(f32[2,8,256,128]{3,2,1,0:T(8,128)S(1)} %bitcast.67, f32[32768]{0:T(1024)S(1)} %subtract_bitcast_fusion), kind=kOutput, calls=%fused_computation.45 | convolution fusion | flops 101712128 | bytes 4325376 | tf_op jit(solution)/shard_map/ij,bjr->bir/dot_general | solution.py:47
  107.1 1.2 copy-done.9
  108.4 1.3 fusion.16
  109.7 42.7 %all-to-all-done.2 = f32[16,256,128]{2,0,1:T(8,128)} async-done(((f32[16,256,128]{2,0,1:T(8,128)}), f32[16,256,128]{2,0,1:T(8,128)}, u32[]{:S(2)}, u32[]{:S(2)}) %all-to-all-start.2) | async-done | bytes 2097184 | tf_op jit(solution)/shard_map/all_to_all | solution.py:121
  152.3 3.4 %all-to-all-start.1 = ((f32[1,256,128]{2,0,1:T(1,128)}), f32[1,256,128]{2,0,1:T(1,128)S(1)}, u32[]{:S(2)}, u32[]{:S(2)}) async-start(f32[1,256,128]{2,0,1:T(1,128)} %bitcast.14), calls=%async_computation.1 | async-start | bytes 262144 | tf_op jit(solution)/shard_map/all_to_all | solution.py:102
  155.7 3.5 %copy.38 = f32[8,16,32,128]{3,2,1,0:T(8,128)} copy(f32[8,16,32,128]{3,1,2,0:T(8,128)} %bitcast.18) | data formatting | bytes 4194304 | tf_op jit(solution)/shard_map/all_to_all | solution.py:121
  159.3 3.1 %all-to-all-done.1 = f32[1,256,128]{2,0,1:T(1,128)S(1)} async-done(((f32[1,256,128]{2,0,1:T(1,128)}), f32[1,256,128]{2,0,1:T(1,128)S(1)}, u32[]{:S(2)}, u32[]{:S(2)}) %all-to-all-start.1) | async-done | bytes 131104 | tf_op jit(solution)/shard_map/all_to_all | solution.py:102
  162.4 6.9 %all-to-all-start.3 = ((f32[128,32,128]{2,1,0:T(8,128)}), f32[128,32,128]{2,1,0:T(8,128)S(1)}, u32[]{:S(2)}, u32[]{:S(2)}) async-start(f32[128,32,128]{2,1,0:T(8,128)} %bitcast.19), calls=%async_computation.3 | async-start | bytes 4194304 | tf_op jit(solution)/shard_map/all_to_all | solution.py:122
  169.4 0.6 negate_exponential_fusion
  170.0 0.6 fusion.41
  170.6 23.3 %all-to-all-done.3 = f32[128,32,128]{2,1,0:T(8,128)S(1)} async-done(((f32[128,32,128]{2,1,0:T(8,128)}), f32[128,32,128]{2,1,0:T(8,128)S(1)}, u32[]{:S(2)}, u32[]{:S(2)}) %all-to-all-start.3) | async-done | bytes 2097184 | tf_op jit(solution)/shard_map/all_to_all | solution.py:122
  193.9 1.6 copy.51
  (40 shorter events, 1.5 us)
Async XLA Ops:
  0.6 35.5 %copy-start = (s32[256,512]{1,0:T(8,128)S(1)}, s32[256,512]{1,0:T(8,128)}, u32[]{:S(2)}) copy-start(s32[256,512]{1,0:T(8,128)} %param.12) | copy-start | bytes 1572868
  4.1 14.3 %copy-start.5 = (f32[16,256,128]{2,1,0:T(8,128)}, f32[16,256,128]{2,1,0:T(8,128)S(1)}, u32[]{:S(2)}) copy-start(f32[16,256,128]{2,1,0:T(8,128)S(1)} %get-tuple-element.36) | copy-start | bytes 6291460
  18.5 1.3 copy-start.3
  19.8 18.1 %collective-permute-start.2 = (f32[2,256,128]{2,1,0:T(8,128)S(1)}, f32[2,256,128]{2,1,0:T(8,128)S(1)}, u32[]{:S(2)}, u32[]{:S(2)}) collective-permute-start(f32[2,256,128]{2,1,0:T(8,128)S(1)} %slice.105), channel_id=1, source_target_pairs={{1,0},{2,1},{3,2},{4,3},{5,4},{6,5},{7,6},{9,8},{10,9},{11,10},{12... | collective-permute-start | bytes 786440 | tf_op jit(solution)/shard_map/ppermute | solution.py:12
  33.6 2.6 %copy-start.12 = (f32[3,16]{1,0:T(4,128)S(1)}, f32[3,16]{1,0:T(4,128)}, u32[]{:S(2)}) copy-start(f32[3,16]{1,0:T(4,128)} %param.13) | copy-start | bytes 580
  34.8 8.5 %collective-permute-start = (f32[2,256,128]{2,1,0:T(8,128)}, f32[2,256,128]{2,1,0:T(8,128)S(1)}, u32[]{:S(2)}, u32[]{:S(2)}) collective-permute-start(f32[2,256,128]{2,1,0:T(8,128)} %slice.74), channel_id=1, source_target_pairs={{1,0},{2,1},{3,2},{4,3},{5,4},{6,5},{7,6},{9,8},{10,9},{11,10},{12... | collective-permute-start | bytes 786440 | tf_op jit(solution)/shard_map/ppermute | solution.py:12
  41.7 2.5 %copy-start.6 = (f32[16,256,128]{2,1,0:T(8,128)S(1)}, f32[16,256,128]{2,1,0:T(8,128)}, u32[]{:S(2)}) copy-start(f32[16,256,128]{2,1,0:T(8,128)} %copy-done.5) | copy-start | bytes 6291460
  44.4 2.2 %copy-start.2 = (f32[18,256,128]{2,1,0:T(8,128)}, f32[18,256,128]{2,1,0:T(8,128)S(1)}, u32[]{:S(2)}) copy-start(f32[18,256,128]{2,1,0:T(8,128)S(1)} %pad_maximum_fusion) | copy-start | bytes 7077892
  50.9 11.4 %collective-permute-start.3 = (f32[18,258,1]{1,2,0:T(1,128)S(1)}, f32[18,258,1]{1,2,0:T(1,128)S(1)}, u32[]{:S(2)}, u32[]{:S(2)}) collective-permute-start(f32[18,258,1]{1,2,0:T(1,128)S(1)} %copy.33), channel_id=1, source_target_pairs={{8,0},{16,8},{24,16},{9,1},{17,9},{25,17},{10,2},{18,10},{26,18},{... | collective-permute-start | bytes 55736 | tf_op jit(solution)/shard_map/ppermute | solution.py:12
  54.9 5.3 %copy-start.7 = (f32[16,256,128]{2,1,0:T(8,128)S(1)}, f32[16,256,128]{2,1,0:T(8,128)}, u32[]{:S(2)}) copy-start(f32[16,256,128]{2,1,0:T(8,128)} %copy-done.5) | copy-start | bytes 6291460
  54.9 11.8 %collective-permute-start.1 = (f32[18,258,1]{1,2,0:T(1,128)S(1)}, f32[18,258,1]{1,2,0:T(1,128)S(1)}, u32[]{:S(2)}, u32[]{:S(2)}) collective-permute-start(f32[18,258,1]{1,2,0:T(1,128)S(1)} %copy.30), channel_id=1, source_target_pairs={{8,0},{16,8},{24,16},{9,1},{17,9},{25,17},{10,2},{18,10},{26,18},{... | collective-permute-start | bytes 55736 | tf_op jit(solution)/shard_map/ppermute | solution.py:12
  66.8 4.3 %copy-start.10 = (f32[1,256,128]{2,0,1:T(1,128)S(1)}, f32[1,256,128]{2,0,1:T(1,128)}, u32[]{:S(2)}) copy-start(f32[1,256,128]{2,0,1:T(1,128)} %get-tuple-element.40) | copy-start | bytes 393220
  66.8 4.3 %copy-start.11 = (f32[1,256,128]{2,0,1:T(1,128)S(1)}, f32[1,256,128]{2,0,1:T(1,128)}, u32[]{:S(2)}) copy-start(f32[1,256,128]{2,0,1:T(1,128)} %get-tuple-element.41) | copy-start | bytes 393220
  83.2 9.0 %copy-start.4 = (f32[16,256,128]{2,1,0:T(8,128)S(1)}, f32[16,256,128]{2,1,0:T(8,128)}, u32[]{:S(2)}) copy-start(f32[16,256,128]{2,1,0:T(8,128)} %copy-done.3) | copy-start | bytes 6291460
  85.5 13.4 %all-to-all-start = ((f32[1,256,128]{2,0,1:T(1,128)}), f32[1,256,128]{2,0,1:T(1,128)S(1)}, u32[]{:S(2)}, u32[]{:S(2)}) async-start(f32[1,256,128]{2,0,1:T(1,128)} %bitcast.7), calls=%async_computation | async-start | bytes 262144 | tf_op jit(solution)/shard_map/all_to_all | solution.py:103
  94.7 9.5 %copy-start.8 = (f32[16,256,128]{2,1,0:T(8,128)S(1)}, f32[16,256,128]{2,1,0:T(8,128)}, u32[]{:S(2)}) copy-start(f32[16,256,128]{2,1,0:T(8,128)} %get-tuple-element.38) | copy-start | bytes 6291460
  98.9 53.4 %all-to-all-start.2 = ((f32[16,256,128]{2,0,1:T(8,128)}), f32[16,256,128]{2,0,1:T(8,128)}, u32[]{:S(2)}, u32[]{:S(2)}) async-start(f32[16,256,128]{2,0,1:T(8,128)} %copy.36), calls=%async_computation.2 | async-start | bytes 4194304 | tf_op jit(solution)/shard_map/all_to_all | solution.py:121
  106.7 1.7 copy-start.9
  152.3 10.1 %all-to-all-start.1 = ((f32[1,256,128]{2,0,1:T(1,128)}), f32[1,256,128]{2,0,1:T(1,128)S(1)}, u32[]{:S(2)}, u32[]{:S(2)}) async-start(f32[1,256,128]{2,0,1:T(1,128)} %bitcast.14), calls=%async_computation.1 | async-start | bytes 262144 | tf_op jit(solution)/shard_map/all_to_all | solution.py:102
  162.4 31.5 %all-to-all-start.3 = ((f32[128,32,128]{2,1,0:T(8,128)}), f32[128,32,128]{2,1,0:T(8,128)S(1)}, u32[]{:S(2)}, u32[]{:S(2)}) async-start(f32[128,32,128]{2,1,0:T(8,128)} %bitcast.19), calls=%async_computation.3 | async-start | bytes 4194304 | tf_op jit(solution)/shard_map/all_to_all | solution.py:122
  169.4 26.2 %copy-start.1 = (s32[256,512]{1,0:T(8,128)S(1)}, s32[256,512]{1,0:T(8,128)}, u32[]{:S(2)}) copy-start(s32[256,512]{1,0:T(8,128)} %param.12) | copy-start | bytes 1572868
where the time goes:
time: 197 us; the launch traced here: 196 us
  waiting for transfers between devices  73.3 us (37%)
  local copies, waits for them, and re-layouts  47.3 us (24%)
  other arithmetic  30.4 us (15%)
  starting transfers between devices  26.8 us (14%)
  blocking collectives  9.72 us (5%)
  matrix products  7 us (4%)
    all_to_all x1, waiting for transfers between devices, local(): lax.all_to_all(lit, 'screen', split_axis=1, concat_axis=0, tiled=True)  42.7 us
    all_to_all x1, waiting for transfers between devices, local(): lax.all_to_all(lit_cam, 'light', split_axis=0, concat_axis=2, tiled=True)  23.3 us
    add x1, other arithmetic, resample(): mixed = near + light_w * (further - near)  12 us
    reshape x1, local copies, waits for them, and re-layouts, local(): density.reshape(bricks_b, BRICK, bricks_a, BRICK, bricks_l, BRICK)  10.6 us
    all_gather x1, blocking collectives, carried_in(): gathered = lax.all_gather(part, axis)  9.72 us
    slice x4, local copies, waits for them, and re-layouts, march_slabs(): tails = passed_along((dens_ext[:, :, :1], lit_ext[:, :, :1]), 'light', -1)  8.64 us
    all_to_all x1, starting transfers between devices, local(): lax.all_to_all(lit_cam, 'light', split_axis=0, concat_axis=2, tiled=True)  6.94 us
    all_to_all x1, starting transfers between devices, march_slabs(): lax.all_to_all(total[None], 'screen', split_axis=1, concat_axis=0, tiled=...  6.67 us
  transfers between devices with their start and end apart: 8, of which 4 were waited for; matrix products, arithmetic and copies ran while one was open for 24% of the time, Pallas kernels for 0%

commit v1 on v0

--- a/solution.py
+++ b/solution.py
@@ -106,6 +106,18 @@
 
 
 def local(density, albedo, light_in, occupancy, phase, fractions):
+
+    def use_slices_by_axis(field_in, row_dim, axis_k):
+        return jnp.concatenate(
+            jax.lax.all_to_all(
+                jnp.stack(jnp.split(field_in, jax.lax.axis_size("light"), axis=row_dim)),
+                axis_name="light",
+                split_axis=0,
+                concat_axis=0,
+            ),
+            axis_k,
+        )
+
     slab_b, width_a, slab_l = density.shape
     bricks_b, bricks_a, bricks_l = occupancy.shape
     masked = (
@@ -119,7 +131,7 @@
     incoming = lax.dynamic_slice_in_dim(light_in, screen_idx * slab_b, slab_b, 0)
     lit = albedo * incoming[:, :, None] * jnp.exp(-(local_depth + before[:, :, None]))
     lit_cam = lax.all_to_all(lit, "screen", split_axis=1, concat_axis=0, tiled=True)
-    lit_cam = lax.all_to_all(lit_cam, "light", split_axis=0, concat_axis=2, tiled=True)
+    lit_cam = use_slices_by_axis(lit_cam, 0, 2)
     picture, passing = march_slabs(masked, lit, phase, fractions)
     return (picture, passing, lit_cam)
 

time: 197 us -> 177 us (0.90)
  waiting for transfers between devices: 73.3 us -> 29.2 us
  starting transfers between devices: 26.8 us -> 51.8 us
  local copies, waits for them, and re-layouts: 47.3 us -> 43.7 us
  other arithmetic: 30.4 us -> 33.4 us
    all_to_all x1, waiting for transfers between devices: 42.7 us -> 0.01 us  [local(): lax.all_to_all(lit, 'screen', split_axis=1, concat_axis=0, tiled=True)]
    all_to_all x1, starting transfers between devices: 6.67 us -> 31 us  [march_slabs(): lax.all_to_all(total[None], 'screen', split_axis=1, concat_axis=0, tiled=...]
    all_to_all x1, waiting for transfers between devices: 4.2 us -> 0.18 us  [march_slabs(): lax.all_to_all(total[None], 'screen', split_axis=1, concat_axis=0, tiled=...]
    reduce_sum x1, other arithmetic: 1.29 us -> 4.3 us  [composite(): jnp.sum(jnp.exp(-screened) * (1.0 - jnp.exp(-extinct)) * shaded, axis=0)]
    all_to_all x1, starting transfers between devices: 6.94 us -> 4.63 us  [use_slices_by_axis(): jax.lax.all_to_all(jnp.stack(jnp.split(field_in, jax.lax.axis_size('light...]
    reshape x1, local copies, waits for them, and re-layouts: 10.6 us -> 8.47 us  [local(): density.reshape(bricks_b, BRICK, bricks_a, BRICK, bricks_l, BRICK)]
  transfers between devices with their start and end apart: 8 -> 8, of which waited for: 4 -> 3; matrix products, arithmetic and copies ran while one was open for 24% -> 41% of each run, Pallas kernels for 0% -> 0%
where the time goes in v1:
time: 177 us; the launch traced here: 176 us
  starting transfers between devices  51.8 us (29%)
  local copies, waits for them, and re-layouts  43.7 us (25%)
  other arithmetic  33.4 us (19%)
  waiting for transfers between devices  29.2 us (16%)
  blocking collectives  9.72 us (5%)
  matrix products  7 us (4%)
    all_to_all x1, starting transfers between devices, march_slabs(): lax.all_to_all(total[None], 'screen', split_axis=1, concat_axis=0, tiled=...  31 us
    all_to_all x1, waiting for transfers between devices, use_slices_by_axis(): jax.lax.all_to_all(jnp.stack(jnp.split(field_in, jax.lax.axis_size('light...  24.1 us
    add x1, other arithmetic, resample(): mixed = near + light_w * (further - near)  11.8 us
    all_gather x1, blocking collectives, carried_in(): gathered = lax.all_gather(part, axis)  9.72 us
    slice x4, local copies, waits for them, and re-layouts, march_slabs(): tails = passed_along((dens_ext[:, :, :1], lit_ext[:, :, :1]), 'light', -1)  8.67 us
    reshape x1, local copies, waits for them, and re-layouts, local(): density.reshape(bricks_b, BRICK, bricks_a, BRICK, bricks_l, BRICK)  8.47 us
    all_to_all x1, starting transfers between devices, local(): lax.all_to_all(lit, 'screen', split_axis=1, concat_axis=0, tiled=True)  5.75 us
    ppermute x4, starting transfers between devices, passed_along(): return lax.ppermute(value, axis, pairs)  5.47 us
  transfers between devices with their start and end apart: 8, of which 3 were waited for; matrix products, arithmetic and copies ran while one was open for 41% of the time, Pallas kernels for 0%

profile of v1, /device:TPU:0, one launch (start us, length us, event | category | flops | bytes accessed | tf_op | source)
XLA Modules:
  0.0 175.8 jit_solution(2172555163234582554)
XLA Ops:
  0.7 0.7 convert_bitcast_fusion
  1.6 0.3 mul.121
  1.9 2.2 %fusion.35 = (f32[16,256]{1,0:T(8,128)S(1)}, f32[16,256,128]{2,1,0:T(8,128)S(1)}) fusion(f32[16,256,128]{2,1,0:T(8,128)} %param.8, f32[256,128]{1,0:T(8,128)S(1)} %mul.121), kind=kLoop, calls=%fused_computation.63 | loop fusion | flops 1044480 | bytes 4341760 | tf_op jit(solution)/shard_map/reduce_sum | solution.py:35
  4.2 9.7 %all-gather = f32[64,256]{1,0:T(8,128)S(1)} all-gather(f32[16,256]{1,0:T(8,128)S(1)} %get-tuple-element.35), channel_id=2, replica_groups=mesh['light'=4,'screen'=8] {'light'}, dimensions={0}, use_global_device_ids=true | all-gather | bytes 81920 | tf_op jit(solution)/shard_map/all_gather | solution.py:17
  13.9 0.7 constant_dynamic-slice_fusion
  14.6 3.8 %exponential_multiply_fusion = f32[16,256,128]{2,1,0:T(8,128)S(1)} fusion(f32[16,256,128]{2,1,0:T(8,128)} %param.9, f32[16,256,128]{2,1,0:T(8,128)S(1)} %get-tuple-element.36, f32[16,256]{1,0:T(8,128)S(1)} %get-tuple-element.26, f32[16,256]{1,0:T(8,128)S(1)} %sub.66, f32[16,256]{1,0:T(8,128)S(1)} %constant_dynamic-slice_fusion), kind=kOutput, calls=%fused_computation.43 | convolution fusion | flops 807944192 | bytes 6340608 | tf_op jit(solution)/shard_map/dot_general | solution.py:34
  18.5 1.3 collective-permute-start.2
  19.8 2.5 %copy.36 = f32[16,256,128]{2,0,1:T(8,128)} copy(f32[16,256,128]{2,1,0:T(8,128)S(1)} %exponential_multiply_fusion) | data formatting | bytes 4194304 | tf_op jit(solution)/shard_map/mul | solution.py:132
  22.4 5.7 %all-to-all-start.2 = ((f32[16,256,128]{2,0,1:T(8,128)}), f32[16,256,128]{2,0,1:T(8,128)}, u32[]{:S(2)}, u32[]{:S(2)}) async-start(f32[16,256,128]{2,0,1:T(8,128)} %copy.36), calls=%async_computation.2 | async-start | bytes 4194304 | tf_op jit(solution)/shard_map/all_to_all | solution.py:133
  28.1 8.5 %reshape.96 = f32[1,16,16,16,8,16]{5,4,3,2,1,0:T(8,128)} reshape(f32[16,256,128]{2,1,0:T(8,128)S(1)} %copy-done.8) | data formatting | bytes 4194304 | tf_op jit(solution)/shard_map/reshape | solution.py:124
  36.6 1.9 %slice_multiply_fusion = f32[1,2,16,16,8,16]{5,4,3,2,1,0:T(8,128)S(1)} fusion(f32[1,16,16,16,8,16]{5,4,3,2,1,0:T(8,128)} %reshape.96, f32[16,8]{1,0:T(8,128)S(1)} %copy.28), kind=kLoop, calls=%fused_computation.41 | loop fusion | flops 65536 | bytes 524800 | tf_op jit(solution)/shard_map/mul | solution.py:124
  38.5 1.3 slice.78
  39.7 1.3 collective-permute-start
  41.1 0.7 fusion.27
  41.8 1.0 fusion.39
  42.8 1.7 pad_maximum_fusion.1
  44.5 1.7 pad_slice_fusion.3
  46.2 2.7 %copy.33 = f32[18,258,1]{1,2,0:T(1,128)S(1)} copy(f32[18,258,1]{2,1,0:T(8,128)} %pad_slice_fusion.3) | data formatting | bytes 37152 | tf_op jit(solution)/shard_map/slice | solution.py:95
  48.9 1.3 collective-permute-start.3
  50.2 1.7 pad_maximum_fusion
  51.9 1.5 copy-done.2
  53.4 1.6 pad_slice_fusion.5
  55.0 2.7 %copy.30 = f32[18,258,1]{1,2,0:T(1,128)S(1)} copy(f32[18,258,1]{2,1,0:T(8,128)} %pad_slice_fusion.5) | data formatting | bytes 37152 | tf_op jit(solution)/shard_map/slice | solution.py:95
  57.7 1.6 collective-permute-start.1
  59.3 2.2 %pad_slice_fusion.2 = f32[18,256,127]{2,1,0:T(8,128)} fusion(f32[18,256,128]{2,1,0:T(8,128)S(1)} %pad_maximum_fusion.1), kind=kLoop, calls=%fused_computation.25 | loop fusion | bytes 4700160 | tf_op jit(solution)/shard_map/slice | solution.py:65
  61.5 2.1 %pad_slice_fusion.4 = f32[18,256,127]{2,1,0:T(8,128)} fusion(f32[18,256,128]{2,1,0:T(8,128)S(1)} %copy-done.3), kind=kLoop, calls=%fused_computation.27 | loop fusion | bytes 4700160 | tf_op jit(solution)/shard_map/slice | solution.py:65
  63.6 2.1 %fusion.3 = f32[18,256,127]{2,1,0:T(8,128)} fusion(f32[2,256,128]{2,1,0:T(8,128)S(1)} %collective-permute-done.2, f32[16,256,128]{2,1,0:T(8,128)S(1)} %copy-done.5), kind=kLoop, calls=%fused_computation.9 | loop fusion | flops 585216 | bytes 4700160 | tf_op jit(solution)/shard_map/concatenate | solution.py:94
  65.8 2.1 %fusion.4 = f32[18,256,127]{2,1,0:T(8,128)} fusion(f32[2,256,128]{2,1,0:T(8,128)S(1)} %collective-permute-done, f32[16,256,128]{2,1,0:T(8,128)S(1)} %copy-done.7), kind=kLoop, calls=%fused_computation.10 | loop fusion | flops 585216 | bytes 4700160 | tf_op jit(solution)/shard_map/concatenate | solution.py:93
  68.0 2.1 %copy.35 = f32[18,256,1]{2,1,0:T(8,128)} copy(f32[18,256,1]{1,2,0:T(1,128)S(1)} %get-tuple-element.48) | data formatting | bytes 36864 | tf_op jit(solution)/shard_map/slice | solution.py:63
  70.1 2.1 %copy.34 = f32[18,256,1]{2,1,0:T(8,128)} copy(f32[18,256,1]{1,2,0:T(1,128)S(1)} %get-tuple-element.49) | data formatting | bytes 36864 | tf_op jit(solution)/shard_map/slice | solution.py:62
  72.4 2.1 %copy.32 = f32[18,256,1]{2,1,0:T(8,128)} copy(f32[18,256,1]{1,2,0:T(1,128)S(1)} %get-tuple-element.50) | data formatting | bytes 36864 | tf_op jit(solution)/shard_map/slice | solution.py:63
  74.5 2.2 %copy.31 = f32[18,256,1]{2,1,0:T(8,128)} copy(f32[18,256,1]{1,2,0:T(1,128)S(1)} %get-tuple-element.51) | data formatting | bytes 36864 | tf_op jit(solution)/shard_map/slice | solution.py:62
  76.7 11.8 %fusion.14 = (f32[18,256,128]{2,1,0:T(8,128)}, f32[18,256,128]{2,1,0:T(8,128)S(1)}) fusion(f32[18,256,1]{2,1,0:T(8,128)} %copy.34, f32[18,256,127]{2,1,0:T(8,128)} %fusion.3, f32[18,256,1]{2,1,0:T(8,128)} %copy.35, f32[18,256,127]{2,1,0:T(8,128)} %pad_slice_fusion.2, f32[18,256,128]{2,1,0:T(8,128)S(1)} %pad_maximum_fusion.1, f32[256,128]{1,0:T(8,128)S(1)} %bitcast.79, ...), kind=kLoop, calls=%fused_computation.24 | loop fusion | flops 12976128 | bytes 19136512 | tf_op jit(solution)/shard_map/add | solution.py:71
  88.5 1.1 fusion.36
  89.6 0.9 subtract_bitcast_fusion
  90.5 2.5 %fusion.24 = f32[2,8,256,128]{3,1,2,0:T(8,128)S(1)} fusion(f32[2,8,256,128]{3,2,1,0:T(8,128)S(1)} %bitcast.69, f32[32768]{0:T(1024)S(1)} %subtract_bitcast_fusion), kind=kOutput, calls=%fused_computation.46 | convolution fusion | flops 101712128 | bytes 4325376 | tf_op jit(solution)/shard_map/ij,bjr->bir/dot_general | solution.py:47
  93.0 1.7 copy.45
  94.7 31.0 %all-to-all-start = ((f32[1,256,128]{2,0,1:T(1,128)}), f32[1,256,128]{2,0,1:T(1,128)S(1)}, u32[]{:S(2)}, u32[]{:S(2)}) async-start(f32[1,256,128]{2,0,1:T(1,128)} %bitcast.7), calls=%async_computation | async-start | bytes 262144 | tf_op jit(solution)/shard_map/all_to_all | solution.py:103
  125.7 4.3 %fusion.16 = f32[256,128]{1,0:T(8,128)} fusion(f32[2,8,256,128]{3,2,1,0:T(8,128)} %copy.45, f32[18,256,128]{2,1,0:T(8,128)} %get-tuple-element.46, f32[16,256,128]{2,1,0:T(8,128)S(1)} %get-tuple-element.38, f32[256,128]{1,0:T(8,128)S(1)} %bitcast.78), kind=kLoop, calls=%fused_computation.31 | loop fusion | flops 4161536 | bytes 8650752 | tf_op jit(solution)/shard_map/reduce_sum | solution.py:79
  130.0 2.3 %copy.37 = f32[16,256,128]{2,1,0:T(8,128)S(1)} copy(f32[16,256,128]{2,0,1:T(8,128)} %all-to-all-done.2) | data formatting | bytes 4194304 | tf_op jit(solution)/shard_map/all_to_all | solution.py:133
  132.5 4.9 %all-to-all-start.1 = ((f32[1,256,128]{2,0,1:T(1,128)}), f32[1,256,128]{2,0,1:T(1,128)S(1)}, u32[]{:S(2)}, u32[]{:S(2)}) async-start(f32[1,256,128]{2,0,1:T(1,128)} %bitcast.14), calls=%async_computation.1 | async-start | bytes 262144 | tf_op jit(solution)/shard_map/all_to_all | solution.py:102
  137.8 1.5 pad_maximum_fusion.4
  139.3 4.9 %all-to-all-done.1 = f32[1,256,128]{2,0,1:T(1,128)S(1)} async-done(((f32[1,256,128]{2,0,1:T(1,128)}), f32[1,256,128]{2,0,1:T(1,128)S(1)}, u32[]{:S(2)}, u32[]{:S(2)}) %all-to-all-start.1) | async-done | bytes 131104 | tf_op jit(solution)/shard_map/all_to_all | solution.py:102
  144.2 4.6 %all-to-all-start.3 = ((f32[4,32,32,128]{3,2,1,0:T(8,128)}), f32[4,32,32,128]{3,2,1,0:T(8,128)S(1)}, u32[]{:S(2)}, u32[]{:S(2)}) async-start(f32[4,32,32,128]{3,2,1,0:T(8,128)} %pad_maximum_fusion.4), calls=%async_computation.3 | async-start | bytes 4194304 | tf_op jit(solution)/shard_map/all_to_all | solution.py:112
  148.8 0.6 negate_exponential_fusion
  149.4 0.6 fusion.42
  150.1 24.1 %all-to-all-done.3 = f32[4,32,32,128]{3,2,1,0:T(8,128)S(1)} async-done(((f32[4,32,32,128]{3,2,1,0:T(8,128)}), f32[4,32,32,128]{3,2,1,0:T(8,128)S(1)}, u32[]{:S(2)}, u32[]{:S(2)}) %all-to-all-start.3) | async-done | bytes 2097184 | tf_op jit(solution)/shard_map/all_to_all | solution.py:112
  174.2 1.6 copy_bitcast_fusion
  (44 shorter events, 1.0 us)
Async XLA Ops:
  0.6 40.4 %copy-start = (s32[256,512]{1,0:T(8,128)S(1)}, s32[256,512]{1,0:T(8,128)}, u32[]{:S(2)}) copy-start(s32[256,512]{1,0:T(8,128)} %param.12) | copy-start | bytes 1572868
  4.1 14.3 %copy-start.6 = (f32[16,256,128]{2,1,0:T(8,128)}, f32[16,256,128]{2,1,0:T(8,128)S(1)}, u32[]{:S(2)}) copy-start(f32[16,256,128]{2,1,0:T(8,128)S(1)} %get-tuple-element.36) | copy-start | bytes 6291460
  18.5 1.3 copy-start.4
  18.5 24.3 %collective-permute-start.2 = (f32[2,256,128]{2,1,0:T(8,128)S(1)}, f32[2,256,128]{2,1,0:T(8,128)S(1)}, u32[]{:S(2)}, u32[]{:S(2)}) collective-permute-start(f32[2,256,128]{2,1,0:T(8,128)S(1)} %slice.109), channel_id=1, source_target_pairs={{1,0},{2,1},{3,2},{4,3},{5,4},{6,5},{7,6},{9,8},{10,9},{11,10},{12... | collective-permute-start | bytes 786440 | tf_op jit(solution)/shard_map/ppermute | solution.py:12
  22.4 5.8 %copy-start.8 = (f32[16,256,128]{2,1,0:T(8,128)S(1)}, f32[16,256,128]{2,1,0:T(8,128)}, u32[]{:S(2)}) copy-start(f32[16,256,128]{2,1,0:T(8,128)} %param.8) | copy-start | bytes 6291460
  22.4 72.3 %all-to-all-start.2 = ((f32[16,256,128]{2,0,1:T(8,128)}), f32[16,256,128]{2,0,1:T(8,128)}, u32[]{:S(2)}, u32[]{:S(2)}) async-start(f32[16,256,128]{2,0,1:T(8,128)} %copy.36), calls=%async_computation.2 | async-start | bytes 4194304 | tf_op jit(solution)/shard_map/all_to_all | solution.py:133
  38.5 2.6 %copy-start.11 = (f32[3,16]{1,0:T(4,128)S(1)}, f32[3,16]{1,0:T(4,128)}, u32[]{:S(2)}) copy-start(f32[3,16]{1,0:T(4,128)} %param.13) | copy-start | bytes 580
  39.7 10.4 %collective-permute-start = (f32[2,256,128]{2,1,0:T(8,128)}, f32[2,256,128]{2,1,0:T(8,128)S(1)}, u32[]{:S(2)}, u32[]{:S(2)}) collective-permute-start(f32[2,256,128]{2,1,0:T(8,128)} %slice.78), channel_id=1, source_target_pairs={{1,0},{2,1},{3,2},{4,3},{5,4},{6,5},{7,6},{9,8},{10,9},{11,10},{12... | collective-permute-start | bytes 786440 | tf_op jit(solution)/shard_map/ppermute | solution.py:12
  48.9 19.0 %collective-permute-start.3 = (f32[18,258,1]{1,2,0:T(1,128)S(1)}, f32[18,258,1]{1,2,0:T(1,128)S(1)}, u32[]{:S(2)}, u32[]{:S(2)}) collective-permute-start(f32[18,258,1]{1,2,0:T(1,128)S(1)} %copy.33), channel_id=1, source_target_pairs={{8,0},{16,8},{24,16},{9,1},{17,9},{25,17},{10,2},{18,10},{26,18},{... | collective-permute-start | bytes 55736 | tf_op jit(solution)/shard_map/ppermute | solution.py:12
  51.9 1.5 copy-start.2
  57.7 3.8 %copy-start.3 = (f32[18,256,128]{2,1,0:T(8,128)S(1)}, f32[18,256,128]{2,1,0:T(8,128)}, u32[]{:S(2)}) copy-start(f32[18,256,128]{2,1,0:T(8,128)} %copy-done.2) | copy-start | bytes 7077892
  57.7 14.5 %collective-permute-start.1 = (f32[18,258,1]{1,2,0:T(1,128)S(1)}, f32[18,258,1]{1,2,0:T(1,128)S(1)}, u32[]{:S(2)}, u32[]{:S(2)}) collective-permute-start(f32[18,258,1]{1,2,0:T(1,128)S(1)} %copy.30), channel_id=1, source_target_pairs={{8,0},{16,8},{24,16},{9,1},{17,9},{25,17},{10,2},{18,10},{26,18},{... | collective-permute-start | bytes 55736 | tf_op jit(solution)/shard_map/ppermute | solution.py:12
  61.5 2.1 %copy-start.5 = (f32[16,256,128]{2,1,0:T(8,128)S(1)}, f32[16,256,128]{2,1,0:T(8,128)}, u32[]{:S(2)}) copy-start(f32[16,256,128]{2,1,0:T(8,128)} %copy-done.4) | copy-start | bytes 6291460
  63.6 2.1 %copy-start.7 = (f32[16,256,128]{2,1,0:T(8,128)S(1)}, f32[16,256,128]{2,1,0:T(8,128)}, u32[]{:S(2)}) copy-start(f32[16,256,128]{2,1,0:T(8,128)} %copy-done.6) | copy-start | bytes 6291460
  72.3 4.4 %copy-start.9 = (f32[1,256,128]{2,0,1:T(1,128)S(1)}, f32[1,256,128]{2,0,1:T(1,128)}, u32[]{:S(2)}) copy-start(f32[1,256,128]{2,0,1:T(1,128)} %get-tuple-element.44) | copy-start | bytes 393220
  72.3 4.4 %copy-start.10 = (f32[1,256,128]{2,0,1:T(1,128)S(1)}, f32[1,256,128]{2,0,1:T(1,128)}, u32[]{:S(2)}) copy-start(f32[1,256,128]{2,0,1:T(1,128)} %get-tuple-element.45) | copy-start | bytes 393220
  94.7 37.8 %all-to-all-start = ((f32[1,256,128]{2,0,1:T(1,128)}), f32[1,256,128]{2,0,1:T(1,128)S(1)}, u32[]{:S(2)}, u32[]{:S(2)}) async-start(f32[1,256,128]{2,0,1:T(1,128)} %bitcast.7), calls=%async_computation | async-start | bytes 262144 | tf_op jit(solution)/shard_map/all_to_all | solution.py:103
  132.5 11.7 %all-to-all-start.1 = ((f32[1,256,128]{2,0,1:T(1,128)}), f32[1,256,128]{2,0,1:T(1,128)S(1)}, u32[]{:S(2)}, u32[]{:S(2)}) async-start(f32[1,256,128]{2,0,1:T(1,128)} %bitcast.14), calls=%async_computation.1 | async-start | bytes 262144 | tf_op jit(solution)/shard_map/all_to_all | solution.py:102
  144.2 30.0 %all-to-all-start.3 = ((f32[4,32,32,128]{3,2,1,0:T(8,128)}), f32[4,32,32,128]{3,2,1,0:T(8,128)S(1)}, u32[]{:S(2)}, u32[]{:S(2)}) async-start(f32[4,32,32,128]{3,2,1,0:T(8,128)} %pad_maximum_fusion.4), calls=%async_computation.3 | async-start | bytes 4194304 | tf_op jit(solution)/shard_map/all_to_all | solution.py:112
  148.8 27.0 %copy-start.1 = (s32[256,512]{1,0:T(8,128)S(1)}, s32[256,512]{1,0:T(8,128)}, u32[]{:S(2)}) copy-start(s32[256,512]{1,0:T(8,128)} %param.12) | copy-start | bytes 1572868
